TPU v7x, 32 devices: a whole 2x2x4 slice. The times are simulated.
32 devices in a mesh: seq: 4 (over z), head: 4 (over y, core), batch: 2 (over x).
Axes of the slice: x: 2, y: 2, z: 4, core: 2. Of those that a mesh axis runs over, the one named last changes fastest.
Arguments:
- tokens: bfloat16 [8192, 2048], P(('batch', 'seq')), parts along dimension 0, may hold values from -6 to 6
- neighbor_bank: bfloat16 [128, 256, 2048], P(('batch', 'seq')), parts along dimension 0, may hold values from -2100 to 2100
- slots: int32 [128], P(('batch', 'seq')), parts along dimension 0, may hold values from 0 to 15
- w_query: bfloat16 [2048, 2048], P('seq', 'head'), may hold values from -0.125 to 0.125
- w_key: bfloat16 [2048, 2048], P('seq', 'head'), may hold values from -0.125 to 0.125
- w_value: bfloat16 [2048, 2048], P('seq', 'head'), may hold values from -0.125 to 0.125
- w_out: bfloat16 [2048, 2048], P('head', 'seq'), may hold values from -0.125 to 0.125
Outputs:
- cross_out: bfloat16 [8192, 2048], P(('batch', 'seq'), 'head'), parts along dimension 0
There are 2 independent parts, one for each index of `batch`. A program takes and returns all parts, laid end to end along the dimension named above; an argument that names none is the same for every part. Nothing has to cross between parts.
Inputs may be any that keep to these rules, and one draw needn't show every extreme that they name: Entry c picks row c // 16 * 16 + slots[c] of neighbor_bank.
All inputs are finite; a program needn't handle non-finite values.
Results may differ from a plain program's by a relative error of at most 0.006.
The roundings to bfloat16 on the way count: a program that leaves them out, or rounds other values in their place, can miss the bound.
Values may be sent and summed in bfloat16 or wider, within the bound.
A program may use at most 128 MiB of HBM per device.

v0:
```python
import math

import jax
import jax.numpy as jnp
from jax import lax
from jax.sharding import PartitionSpec as P

HEAD_DIM = 128


def passed_along(block, axis, distance):
    devices = range(lax.axis_size(axis))
    route = [(i - distance, i) for i in devices if i - distance in devices]
    return lax.ppermute(block, axis, route)


def attend(query_blocks, key_blocks, value_blocks):
    scores = jnp.einsum(
        "cmhd,cnhd->chmn", query_blocks, key_blocks, preferred_element_type=jnp.float32
    ) / math.sqrt(HEAD_DIM)
    peak_score = jnp.max(scores, axis=-1, keepdims=True)
    exponent = jnp.exp(scores - peak_score)
    weights = (exponent / jnp.sum(exponent, axis=-1, keepdims=True)).astype(jnp.bfloat16)
    blended = jnp.einsum(
        "chmn,cnhd->cmhd", weights, value_blocks, preferred_element_type=jnp.float32
    ).astype(jnp.bfloat16)
    return blended.reshape(blended.shape[0] * blended.shape[1], blended.shape[2] * blended.shape[3])


def fold_rows(source, shard_rows):
    return jnp.dot(source, shard_rows, preferred_element_type=jnp.float32)


def local(tokens, neighbor_bank, slots, w_query, w_key, w_value, w_out):
    tok_rows, model_width = tokens.shape
    block_count = neighbor_bank.shape[0]
    neighbor_rows = neighbor_bank.shape[1]
    block_len = tok_rows // block_count
    local_width = w_query.shape[1]
    local_heads = local_width // HEAD_DIM
    hidden = tokens.astype(jnp.float32)
    normed = (hidden * lax.rsqrt(jnp.mean(hidden * hidden, axis=-1, keepdims=True) + 1e-06)).astype(
        jnp.bfloat16
    )
    retrieved = jnp.take(neighbor_bank, slots, axis=0)
    arrived = passed_along(retrieved[block_count - 1], "seq", 1)
    context = jnp.concatenate([arrived[None], retrieved[: block_count - 1]], axis=0)
    context_flat = context.reshape(block_count * neighbor_rows, model_width)
    query_sum = fold_rows(normed, lax.all_gather(w_query, "seq", axis=0, tiled=True))
    key_sum = fold_rows(context_flat, lax.all_gather(w_key, "seq", axis=0, tiled=True))
    value_sum = fold_rows(context_flat, lax.all_gather(w_value, "seq", axis=0, tiled=True))
    query_blocks = query_sum.astype(jnp.bfloat16).reshape(
        block_count, block_len, local_heads, HEAD_DIM
    )
    key_blocks = key_sum.astype(jnp.bfloat16).reshape(
        block_count, neighbor_rows, local_heads, HEAD_DIM
    )
    value_blocks = value_sum.astype(jnp.bfloat16).reshape(
        block_count, neighbor_rows, local_heads, HEAD_DIM
    )
    attended = attend(query_blocks, key_blocks, value_blocks)
    every_head = lax.all_gather(attended, "head", axis=1, tiled=True)
    wide_rows = lax.all_gather(w_out, "seq", axis=1, tiled=True)
    own_columns = lax.all_to_all(wide_rows, "head", split_axis=1, concat_axis=0, tiled=True)
    return jnp.dot(every_head, own_columns, preferred_element_type=jnp.float32).astype(jnp.bfloat16)


def solution(mesh):
    in_specs = (
        P(("batch", "seq"), None),
        P(("batch", "seq"), None, None),
        P(("batch", "seq")),
        P("seq", "head"),
        P("seq", "head"),
        P("seq", "head"),
        P("head", "seq"),
    )
    out_specs = P(("batch", "seq"), "head")
    return jax.shard_map(local, mesh=mesh, in_specs=in_specs, out_specs=out_specs, check_vma=False)
```

profile of v0, /device:TPU:0, one launch (start us, length us, event | category | flops | bytes accessed | tf_op | source)
XLA Modules:
  0.0 271.8 jit_solution(8878170851766473111)
XLA Ops:
  6.5 0.7 all-gather.10.cloned.1.call-update
  7.3 0.7 all-gather.8.cloned.1.call-update
  8.1 0.7 all-gather.6.cloned.1.call-update
  8.8 0.7 compare_select_fusion
  9.4 0.7 compare_and_fusion
  10.1 13.0 %gather_fusion = bf16[16,256,2048]{2,1,0:T(8,128)(2,1)} fusion(bf16[16,256,2048]{2,1,0:T(8,128)(2,1)} %param.8, s32[1024]{0:T(1024)S(1)} %pad_clamp_fusion), kind=kCustom, calls=%fused_computation | custom fusion | bytes 33554496 | tf_op jit(solution)/shard_map/jit(_take)/gather | solution.py:45
  23.1 8.6 %broadcast_select_fusion = bf16[16,256,2048]{2,1,0:T(8,128)(2,1)S(1)} fusion(bf16[16,256,2048]{2,1,0:T(8,128)(2,1)} %gather_fusion, pred[16]{0:T(512)(128)(4,1)S(1)} %compare_and_fusion), kind=kLoop, calls=%fused_computation.3 | loop fusion | flops 8388608 | bytes 33554448 | tf_op jit(solution)/shard_map/jit(_take)/select_n | solution.py:45
  31.7 5.7 %copy-done = bf16[16,256,2048]{2,1,0:T(8,128)(2,1)} copy-done((bf16[16,256,2048]{2,1,0:T(8,128)(2,1)}, bf16[16,256,2048]{2,1,0:T(8,128)(2,1)S(1)}, u32[]{:S(2)}) %copy-start) | copy-done | bytes 16777240
  37.5 5.1 %collective-permute-start = (bf16[256,2048]{1,0:T(8,128)(2,1)S(1)}, bf16[256,2048]{1,0:T(8,128)(2,1)S(1)}, u32[]{:S(2)}, u32[]{:S(2)}) collective-permute-start(bf16[256,2048]{1,0:T(8,128)(2,1)S(1)} %slice_bitcast_fusion), channel_id=1, source_target_pairs={{0,8},{8,16},{16,24},{1,9},{9,17},{17,25},{2,10},{10,18},{18,26},{... | collective-permute-start | bytes 3145736 | tf_op jit(solution)/shard_map/ppermute | solution.py:14
  42.6 1.0 copy.19
  43.7 2.2 copy-done.1
  45.9 0.9 fusion.1
  46.8 31.1 %collective-permute-done = bf16[256,2048]{1,0:T(8,128)(2,1)S(1)} collective-permute-done((bf16[256,2048]{1,0:T(8,128)(2,1)S(1)}, bf16[256,2048]{1,0:T(8,128)(2,1)S(1)}, u32[]{:S(2)}, u32[]{:S(2)}) %collective-permute-start) | collective-permute-done | bytes 1048608 | tf_op jit(solution)/shard_map/ppermute | solution.py:14
  77.9 6.6 %pad_maximum_fusion = bf16[16,256,2048]{2,1,0:T(8,128)(2,1)} fusion(bf16[15,256,2048]{2,1,0:T(8,128)(2,1)S(1)} %slice-done, bf16[1,256,2048]{2,1,0:T(8,128)(2,1)S(1)} %bitcast.28), kind=kLoop, calls=%fused_computation.2 | loop fusion | flops 8388608 | bytes 33554432 | tf_op jit(solution)/shard_map/concatenate | solution.py:47
  84.5 14.4 %convolution_convert_fusion = bf16[4096,512]{1,0:T(8,128)(2,1)} fusion(bf16[4096,2048]{1,0:T(8,128)(2,1)} %bitcast.21, bf16[2048,512]{1,0:T(8,128)(2,1)} %all-gather.10.cloned.1.call-done), kind=kOutput, calls=%fused_computation.8 | convolution fusion | flops 8592031744 | bytes 23068672 | tf_op jit(solution)/shard_map/dot_general | solution.py:31
  98.9 13.7 %all-gather.8.cloned.1.call-done = bf16[2048,512]{1,0:T(8,128)(2,1)} async-done(((bf16[512,512]{1,0:T(8,128)(2,1)}), bf16[2048,512]{1,0:T(8,128)(2,1)}) %all-gather.8.cloned.1.call-update) | async-done | bytes 2097168 | tf_op jit(solution)/shard_map/all_gather | solution.py:49
  112.6 5.2 %fusion.18 = bf16[1024,512]{1,0:T(8,128)(2,1)S(1)} fusion(bf16[2048,512]{1,0:T(8,128)(2,1)} %all-gather.8.cloned.1.call-done, bf16[1024,2048]{1,0:T(8,128)(2,1)} %param.7, f32[1024]{0:T(1024)S(1)} %add_rsqrt_fusion), kind=kOutput, calls=%fused_computation.23 | convolution fusion | flops 2154299392 | bytes 7344128 | tf_op jit(solution)/shard_map/dot_general | solution.py:31
  117.8 7.0 %reshape.36 = bf16[16,256,4,128]{3,2,1,0:T(4,128)(2,1)} reshape(bf16[4096,512]{1,0:T(8,128)(2,1)} %convolution_convert_fusion) | data formatting | bytes 8388608 | tf_op jit(solution)/shard_map/reshape | solution.py:55
  125.1 34.8 %all-gather.6.cloned.1.call-done = bf16[2048,512]{1,0:T(8,128)(2,1)} async-done(((bf16[512,512]{1,0:T(8,128)(2,1)}), bf16[2048,512]{1,0:T(8,128)(2,1)}) %all-gather.6.cloned.1.call-update) | async-done | bytes 2097168 | tf_op jit(solution)/shard_map/all_gather | solution.py:51
  159.9 14.4 %convolution_convert_fusion.1 = bf16[4096,512]{1,0:T(8,128)(2,1)} fusion(bf16[4096,2048]{1,0:T(8,128)(2,1)} %bitcast.22, bf16[2048,512]{1,0:T(8,128)(2,1)} %all-gather.6.cloned.1.call-done), kind=kOutput, calls=%fused_computation.9 | convolution fusion | flops 8592031744 | bytes 23068672 | tf_op jit(solution)/shard_map/dot_general | solution.py:31
  174.3 7.0 %reshape.34 = bf16[16,256,4,128]{3,2,1,0:T(4,128)(2,1)} reshape(bf16[4096,512]{1,0:T(8,128)(2,1)} %convolution_convert_fusion.1) | data formatting | bytes 8388608 | tf_op jit(solution)/shard_map/reshape | solution.py:58
  181.2 3.8 %fusion.7 = f32[16,4,64,256]{3,2,1,0:T(8,128)S(1)} fusion(bf16[16,256,4,128]{3,2,1,0:T(4,128)(2,1)} %reshape.36, bf16[16,64,4,128]{3,2,1,0:T(4,128)(2,1)S(1)} %reshape.35), kind=kOutput, calls=%fused_computation.13 | convolution fusion | flops 268435456 | bytes 9437184 | tf_op jit(solution)/shard_map/cmhd,cnhd->chmn/dot_general | solution.py:18
  185.0 2.0 copy-done.2
  187.0 1.6 fusion.33
  188.6 12.0 %fusion.21 = bf16[16,64,4,128]{3,1,2,0:T(8,128)(2,1)S(1)} fusion(bf16[16,256,4,128]{3,2,1,0:T(4,128)(2,1)} %reshape.34, f32[16,4,64]{2,1,0:T(4,128)S(1)} %fusion.33, f32[16,4,64,256]{3,2,1,0:T(8,128)} %copy-done.2), kind=kOutput, calls=%fused_computation.25 | convolution fusion | flops 274206976 | bytes 9453568 | tf_op jit(solution)/shard_map/chmn,cnhd->cmhd/dot_general | solution.py:24
  200.6 0.9 copy.18
  201.5 1.2 copy.33
  202.7 3.1 %all-gather.14.cloned.1.call-done = bf16[512,2048]{0,1:T(8,128)(2,1)} async-done(((bf16[512,512]{0,1:T(8,128)(2,1)}), bf16[512,2048]{0,1:T(8,128)(2,1)}) %all-gather.14.cloned.1.call-update) | async-done | bytes 2097168 | tf_op jit(solution)/shard_map/all_gather | solution.py:63
  205.8 48.4 %all_to_all.19 = bf16[512,4,512]{0,2,1:T(8,128)(2,1)S(1)} all-to-all(bf16[512,4,512]{0,2,1:T(8,128)(2,1)} %bitcast.26), channel_id=1, replica_groups=mesh['seq'=4,'head'=4,'batch'=2] {'head'}, dimensions={1} | all-to-all | bytes 4194304 | tf_op jit(solution)/shard_map/all_to_all | solution.py:64
  254.2 2.4 copy.20
  256.6 2.6 all-gather.12.cloned.1.call-done
  259.1 6.2 %convolution_convert_fusion.2 = bf16[1024,512]{1,0:T(8,128)(2,1)} fusion(bf16[1024,2048]{1,0:T(8,128)(2,1)} %all-gather.12.cloned.1.call-done, bf16[2048,512]{1,0:T(8,128)(2,1)} %bitcast.27), kind=kOutput, calls=%fused_computation.24 | convolution fusion | flops 2148007936 | bytes 7340032 | tf_op jit(solution)/shard_map/dot_general | solution.py:65
  (19 shorter events, 0.6 us)
Async XLA Ops:
  6.5 77.9 %all-gather.10.cloned.1.call-start = ((), (), s32[]{:S(2)}) async-start(), calls=%async_computation.3 | async-start | bytes 2621440 | tf_op jit(solution)/shard_map/all_gather | solution.py:50
  7.3 105.4 %all-gather.8.cloned.1.call-start = ((), (), s32[]{:S(2)}) async-start(), calls=%async_computation.2 | async-start | bytes 2621440 | tf_op jit(solution)/shard_map/all_gather | solution.py:49
  8.0 151.9 %all-gather.6.cloned.1.call-start = ((), (), s32[]{:S(2)}) async-start(), calls=%async_computation.1 | async-start | bytes 2621440 | tf_op jit(solution)/shard_map/all_gather | solution.py:51
  8.7 197.1 %all-gather.14.cloned.1.call-start = ((), (), s32[]{:S(2)}) async-start(), calls=%async_computation.5 | async-start | bytes 2621440 | tf_op jit(solution)/shard_map/all_gather | solution.py:63
  23.1 19.5 %copy-start.3 = (bf16[512,512]{1,0:T(8,128)(2,1)S(1)}, bf16[512,512]{1,0:T(8,128)(2,1)}, u32[]{:S(2)}) copy-start(bf16[512,512]{1,0:T(8,128)(2,1)} %param.13) | copy-start | bytes 1572868
  31.7 5.7 %copy-start = (bf16[16,256,2048]{2,1,0:T(8,128)(2,1)}, bf16[16,256,2048]{2,1,0:T(8,128)(2,1)S(1)}, u32[]{:S(2)}) copy-start(bf16[16,256,2048]{2,1,0:T(8,128)(2,1)S(1)} %broadcast_select_fusion) | copy-start | bytes 50331652
  37.5 40.4 %collective-permute-start = (bf16[256,2048]{1,0:T(8,128)(2,1)S(1)}, bf16[256,2048]{1,0:T(8,128)(2,1)S(1)}, u32[]{:S(2)}, u32[]{:S(2)}) collective-permute-start(bf16[256,2048]{1,0:T(8,128)(2,1)S(1)} %slice_bitcast_fusion), channel_id=1, source_target_pairs={{0,8},{8,16},{16,24},{1,9},{9,17},{17,25},{2,10},{10,18},{18,26},{... | collective-permute-start | bytes 3145736 | tf_op jit(solution)/shard_map/ppermute | solution.py:14
  43.6 215.5 %all-gather.12.cloned.1.call-start = ((), (), s32[]{:S(2)}) async-start(), calls=%async_computation.4 | async-start | bytes 5242880 | tf_op jit(solution)/shard_map/all_gather | solution.py:62
  43.7 2.2 copy-start.1
  43.7 34.2 %slice-start = ((bf16[16,256,2048]{2,1,0:T(8,128)(2,1)}), bf16[15,256,2048]{2,1,0:T(8,128)(2,1)S(1)}, s32[]{:S(2)}) async-start(bf16[16,256,2048]{2,1,0:T(8,128)(2,1)} %copy-done), calls=%async_computation.6 | async-start | bytes 31457280 | tf_op jit(solution)/shard_map/slice | solution.py:47
  185.0 2.0 copy-start.2
Sparse Core Ops, SparseCore 0:
  8.9 56.2 all-gather.9
  66.7 45.8 all-gather.7
  114.2 45.6 all-gather.5
  161.3 44.4 all-gather.13
  207.2 51.8 all-gather.11
where the time goes:
time: 272 us
  waiting for transfers between devices  87.4 us (32%)
  matrix products  56 us (21%)
  blocking collectives  48.4 us (18%)
  local copies, waits for them, and re-layouts  42.6 us (16%)
  other arithmetic  19 us (7%)
  between operations  13.2 us (5%)
  starting transfers between devices  5.23 us (2%)
    all_to_all x1, blocking collectives, local(): lax.all_to_all(wide_rows, 'head', split_axis=1, concat_axis=0, tiled=True)  48.4 us
    all_gather x1, waiting for transfers between devices, local(): lax.all_gather(w_value, 'seq', axis=0, tiled=True)  34.8 us
    dot_general x3, matrix products, fold_rows(): return jnp.dot(source, shard_rows, preferred_element_type=jnp.float32)  34 us
    ppermute x1, waiting for transfers between devices, passed_along(): return lax.ppermute(block, axis, route)  31.1 us
    all_gather x1, waiting for transfers between devices, local(): lax.all_gather(w_query, 'seq', axis=0, tiled=True)  13.7 us
    gather x1, local copies, waits for them, and re-layouts, local(): retrieved = jnp.take(neighbor_bank, slots, axis=0)  13 us
    unnamed x10, local copies, waits for them, and re-layouts  12.1 us
    dot_general x1, matrix products, attend(): jnp.einsum('chmn,cnhd->cmhd', weights, value_blocks, preferred_element_ty...  12 us
  transfers between devices with their start and end apart: 6, of which 5 were waited for; matrix products, arithmetic and copies ran while one was open for 37% of the time, Pallas kernels for 0%

commit v1 on v0

--- a/solution.py
+++ b/solution.py
@@ -1,11 +1,370 @@
+import functools
 import math
 
 import jax
 import jax.numpy as jnp
 from jax import lax
+from jax.experimental import pallas as pl
+from jax.experimental.pallas import tpu as pltpu
 from jax.sharding import PartitionSpec as P
 
 HEAD_DIM = 128
+F32 = jnp.float32
+BF16 = jnp.bfloat16
+
+
+def fused(S, H, NS, tokens, bank, slots, w_query, w_key, w_value, w_out, out,
+          G, WO, tok, normed, rows_in, kv, qb, halo_out, halo_in, att_own, att, acc,
+          ld_sem, wl_sem, zr, xr, send_r, send_l, send_x, halo_s, halo_r,
+          att_s, att_r, att_l, wo_s, wo_r, wo_xs, wo_xr, wo_l):
+    s, h, b = lax.axis_index("seq"), lax.axis_index("head"), lax.axis_index("batch")
+    nblk, nrow, D = bank.shape
+    T = tokens.shape[0]
+    blk = T // nblk
+    CW = HEAD_DIM
+    RS = w_query.shape[0]
+    RH = RS // 2
+    WH = CW // 2
+
+    def dev(seq, head, batch):
+        return {"seq": seq, "head": head, "batch": batch}
+
+    def rcopy(src, dst, ss, rs, device):
+        return pltpu.make_async_remote_copy(
+            src_ref=src, dst_ref=dst, send_sem=ss, recv_sem=rs,
+            device_id=device, device_id_type=pl.DeviceIdType.MESH)
+
+    w_loads = []
+    for k, w in enumerate((w_query, w_key, w_value)):
+        for j in range(NS):
+            c = pltpu.make_async_copy(
+                w.at[:, pl.ds(j * CW, CW)],
+                G.at[j, pl.ds(s * RS, RS), pl.ds(k * CW, CW)], wl_sem.at[k * NS + j])
+            c.start()
+            w_loads.append(c)
+    tok_load = pltpu.make_async_copy(tokens, tok, ld_sem.at[nblk])
+    tok_load.start()
+    bank_loads = [pltpu.make_async_copy(bank.at[i], rows_in.at[i], ld_sem.at[i]) for i in range(nblk)]
+    for c in bank_loads:
+        c.start()
+
+    barrier = pltpu.get_barrier_semaphore()
+    for i in range(S):
+        for k in range(H):
+            @pl.when(jnp.logical_or(s != i, h != k))
+            def _():
+                pl.semaphore_signal(barrier, inc=1, device_id=dev(i, k, b), device_id_type=pl.DeviceIdType.MESH)
+    pl.semaphore_signal(barrier, inc=1, device_id=dev(s, h, 1 - b), device_id_type=pl.DeviceIdType.MESH)
+    pl.semaphore_wait(barrier, S * H)
+
+    def chunk(t, origin, half):
+        return G.at[t, pl.ds(origin * RS + half * RH, RH), :]
+
+    def right(t, origin):
+        return rcopy(chunk(t, origin, b), chunk(t, origin, b), send_r.at[t, origin], zr.at[t, origin],
+                     dev(lax.rem(s + 1, S), h, b))
+
+    def left(t, origin):
+        return rcopy(chunk(t, origin, b), chunk(t, origin, b), send_l.at[t, origin], zr.at[t, origin],
+                     dev(lax.rem(s + S - 1, S), h, b))
+
+    def twin(t, origin, half):
+        return rcopy(chunk(t, origin, half), chunk(t, origin, half), send_x.at[t, origin], xr.at[t, origin],
+                     dev(s, h, 1 - b))
+
+    def send_own(t):
+        @pl.when(s < S - 1)
+        def _():
+            right(t, s).start()
+
+        @pl.when(s > 0)
+        def _():
+            left(t, s).start()
+
+    def relay(t, d):
+        @pl.when(s >= d)
+        def _():
+            right(t, s - d).wait_recv()
+
+            @pl.when(s < S - 1)
+            def _():
+                right(t, s - d).start()
+            twin(t, s - d, b).start()
+
+        @pl.when(s + d < S)
+        def _():
+            left(t, s + d).wait_recv()
+
+            @pl.when(s > 0)
+            def _():
+                left(t, s + d).start()
+            twin(t, s + d, b).start()
+
+    def wo_part(origin, half):
+        return WO.at[:, pl.ds(origin * CW + half * WH, WH), :]
+
+    def wo_send(dest):
+        return rcopy(w_out.at[:, pl.ds(b * WH, WH), :], wo_part(h, b), wo_s.at[dest], wo_r.at[h],
+                     dev(dest, s, b))
+
+    def wo_twin(origin, half):
+        return rcopy(wo_part(origin, half), wo_part(origin, half), wo_xs.at[origin], wo_xr.at[origin],
+                     dev(s, h, 1 - b))
+
+    wo_own = pltpu.make_async_copy(w_out, WO.at[:, pl.ds(h * CW, CW), :], wo_l)
+
+    def attend(t, first_key, blocks):
+        scores, probs = [], []
+        for c, keys in blocks:
+            q = qb[pl.ds(c * blk, blk), :]
+            k = keys(0)
+            scores.append(lax.dot_general(q, k, (((1,), (1,)), ((), ())), preferred_element_type=F32)
+                          * (1.0 / math.sqrt(HEAD_DIM)))
+        for sc in scores:
+            e = jnp.exp(sc - jnp.max(sc, axis=-1, keepdims=True))
+            probs.append((e / jnp.sum(e, axis=-1, keepdims=True)).astype(BF16))
+        for (c, keys), p in zip(blocks, probs):
+            o = jnp.dot(p, keys(1), preferred_element_type=F32)
+            att_own[t, pl.ds(c * blk, blk), :] = o.astype(BF16)
+
+    def halo(t):
+        return rcopy(halo_out.at[t], halo_in.at[t], halo_s.at[t], halo_r.at[t], dev(lax.rem(s + 1, S), h, b))
+
+    peers = ((h // 2) * 2 + 1 - lax.rem(h, 2), lax.rem(h + 2, H), lax.rem((h // 2) * 2 + 1 - lax.rem(h, 2) + 2, H))
+
+    def att_send(t, k):
+        return rcopy(att_own.at[t], att.at[t, :, pl.ds(h * CW, CW)], att_s.at[t, k], att_r.at[t, k],
+                     dev(s, peers[k], b))
+
+    def att_here(t):
+        return pltpu.make_async_copy(att_own.at[t], att.at[t, :, pl.ds(h * CW, CW)], att_l.at[t])
+
+    per = 4 if nblk % 4 == 0 else 1
+    steps = nblk // per
+
+    def project(t, lo, hi):
+        def one(i, _):
+            rows = rows_in[pl.ds(i * per, per)].reshape(per * nrow, D)
+            kv[pl.ds(i * per, per)] = jnp.dot(
+                rows, G[t, :, pl.ds(CW, 2 * CW)], preferred_element_type=F32).astype(BF16).reshape(per, nrow, 2 * CW)
+            return 0
+        lax.fori_loop(lo, hi, one, 0)
+
+    def queries(t):
+        qb[...] = jnp.dot(normed[...], G[t, :, pl.ds(0, CW)], preferred_element_type=F32).astype(BF16)
+
+    for c in w_loads:
+        c.wait()
+    send_own(0)
+
+    @pl.when(s == 0)
+    def _():
+        halo_in[...] = jnp.zeros_like(halo_in)
+
+    tok_load.wait()
+
+    def norm(i, _):
+        x = tok[pl.ds(i * blk, blk), :].astype(F32)
+        normed[pl.ds(i * blk, blk), :] = (
+            x * lax.rsqrt(jnp.mean(x * x, axis=-1, keepdims=True) + 1e-06)).astype(BF16)
+        return 0
+    lax.fori_loop(0, nblk, norm, 0)
+
+    @pl.when(h == s)
+    def _():
+        wo_own.start()
+    for c in bank_loads:
+        c.wait()
+
+    group = max(g for g in range(1, 6) if (nblk - 1) % g == 0)
+
+    def stage(t, _):
+        @pl.when(t < NS - 1)
+        def _():
+            send_own(t + 1)
+
+        @pl.when(t < S)
+        def _():
+            dest = lax.rem(t * (S - 1), S)
+
+            @pl.when(jnp.logical_or(dest != s, h != s))
+            def _():
+                wo_send(dest).start()
+
+        @pl.when(t < NS)
+        def _():
+            relay(t, 1)
+
+        @pl.when(t == NS)
+        def _():
+            for o in range(H):
+                @pl.when(jnp.logical_or(s != h, h != o))
+                def _():
+                    rcopy(wo_part(o, b), wo_part(o, b), wo_s.at[0], wo_r.at[o], dev(s, h, 1 - b)).wait_recv()
+                    wo_twin(o, b).start()
+
+        @pl.when(t > 0)
+        def _():
+            project(t - 1, 0, steps // 2)
+
+        @pl.when(t < NS)
+        def _():
+            relay(t, 2)
+
+        @pl.when(t > 0)
+        def _():
+            project(t - 1, steps // 2, steps)
+            last = slots[nblk - 1]
+
+            @pl.when(s < S - 1)
+            def _():
+                halo_out[t - 1] = kv[last]
+                halo(t - 1).start()
+            queries(t - 1)
+
+        @pl.when(t < NS)
+        def _():
+            for d in range(3, S):
+                relay(t, d)
+
+        @pl.when(t > 0)
+        def _():
+            u = t - 1
+
+            def some(i, _):
+                blocks = []
+                for g in range(group):
+                    c = 1 + i * group + g
+                    at = slots[c - 1]
+                    blocks.append((c, lambda k, at=at: kv[at, :, k * CW:(k + 1) * CW]))
+                attend(u, None, blocks)
+                return 0
+            lax.fori_loop(0, (nblk - 1) // group, some, 0)
+
+            @pl.when(s > 0)
+            def _():
+                halo(u).wait_recv()
+            attend(u, None, [(0, lambda k: halo_in[u, :, k * CW:(k + 1) * CW])])
+            for k in range(3):
+                att_send(u, k).start()
+            att_here(u).start()
+
+        @pl.when(t < NS)
+        def _():
+            for o in range(S):
+                @pl.when(s != o)
+                def _():
+                    twin(t, o, 1 - b).wait_recv()
+        return 0
+
+    lax.fori_loop(0, NS + 1, stage, 0)
+
+    for o in range(H):
+        @pl.when(jnp.logical_or(s != h, h != o))
+        def _():
+            wo_twin(o, 1 - b).wait_recv()
+
+    @pl.when(h == s)
+    def _():
+        wo_own.wait()
+
+    tile = T // 4
+
+    def fold(j, _):
+        att_here(j).wait()
+        for k in range(3):
+            rcopy(att_own.at[j], att.at[j, :, pl.ds(peers[k] * CW, CW)], att_s.at[j, k], att_r.at[j, k],
+                  dev(s, peers[k], b)).wait_recv()
+
+        def rows(i, _):
+            r = pl.ds(i * tile, tile)
+            part = jnp.dot(att[j, r, :], WO[j], preferred_element_type=F32)
+
+            @pl.when(j == 0)
+            def _():
+                acc[r, :] = part
+
+            @pl.when(jnp.logical_and(j > 0, j < NS - 1))
+            def _():
+                acc[r, :] += part
+
+            @pl.when(j == NS - 1)
+            def _():
+                out[r, :] = (acc[r, :] + part).astype(BF16)
+            return 0
+        lax.fori_loop(0, 4, rows, 0)
+        return 0
+    lax.fori_loop(0, NS, fold, 0)
+
+    def drain(t, _):
+        for d in range(S):
+            @pl.when(jnp.logical_and(s >= d, s < S - 1))
+            def _():
+                right(t, s - d).wait_send()
+
+            @pl.when(jnp.logical_and(s + d < S, s > 0))
+            def _():
+                left(t, s + d).wait_send()
+        for o in range(S):
+            @pl.when(s != o)
+            def _():
+                twin(t, o, b).wait_send()
+
+        @pl.when(s < S - 1)
+        def _():
+            halo(t).wait_send()
+        for k in range(3):
+            att_send(t, k).wait_send()
+        return 0
+    lax.fori_loop(0, NS, drain, 0)
+    for dest in range(S):
+        @pl.when(jnp.logical_or(dest != s, h != s))
+        def _():
+            wo_send(dest).wait_send()
+    for o in range(H):
+        @pl.when(jnp.logical_or(s != h, h != o))
+        def _():
+            wo_twin(o, b).wait_send()
+
+
+def one_kernel(tokens, neighbor_bank, slots, w_query, w_key, w_value, w_out):
+    S, H = lax.axis_size("seq"), lax.axis_size("head")
+    T, D = tokens.shape
+    nblk, nrow = neighbor_bank.shape[:2]
+    width = w_query.shape[1]
+    NS = width // HEAD_DIM
+    CW = HEAD_DIM
+    out_cols = D // H
+    dma = pltpu.SemaphoreType.DMA
+    hbm = pl.BlockSpec(memory_space=pl.ANY)
+    return pl.pallas_call(
+        functools.partial(fused, S, H, NS),
+        out_shape=jax.ShapeDtypeStruct((T, out_cols), BF16),
+        in_specs=[hbm, hbm, pl.BlockSpec(memory_space=pltpu.SMEM), hbm, hbm, hbm, hbm],
+        out_specs=pl.BlockSpec(memory_space=pltpu.VMEM),
+        scratch_shapes=[
+            pltpu.VMEM((NS, D, 3 * CW), BF16),
+            pltpu.VMEM((NS, H * CW, out_cols), BF16),
+            pltpu.VMEM((T, D), BF16),
+            pltpu.VMEM((T, D), BF16),
+            pltpu.VMEM((nblk, nrow, D), BF16),
+            pltpu.VMEM((nblk, nrow, 2 * CW), BF16),
+            pltpu.VMEM((T, CW), BF16),
+            pltpu.VMEM((NS, nrow, 2 * CW), BF16),
+            pltpu.VMEM((NS, nrow, 2 * CW), BF16),
+            pltpu.VMEM((NS, T, CW), BF16),
+            pltpu.VMEM((NS, T, H * CW), BF16),
+            pltpu.VMEM((T, out_cols), F32),
+            dma((nblk + 1,)),
+            dma((3 * NS,)),
+            dma((NS, S)), dma((NS, S)), dma((NS, S)), dma((NS, S)), dma((NS, S)),
+            dma((NS,)), dma((NS,)),
+            dma((NS, 3)), dma((NS, 3)), dma((NS,)),
+            dma((S,)), dma((H,)), dma((H,)), dma((H,)), dma,
+        ],
+        compiler_params=pltpu.CompilerParams(
+            collective_id=0, has_side_effects=True, vmem_limit_bytes=63 * 1024 * 1024),
+    )(tokens, neighbor_bank, slots, w_query, w_key, w_value, w_out.reshape(NS, CW, -1))
 
 
 def passed_along(block, axis, distance):
@@ -76,4 +435,6 @@
         P("head", "seq"),
     )
     out_specs = P(("batch", "seq"), "head")
-    return jax.shard_map(local, mesh=mesh, in_specs=in_specs, out_specs=out_specs, check_vma=False)
+    square = mesh.shape["seq"] == 4 and mesh.shape["head"] == 4 and mesh.shape["batch"] == 2
+    body = one_kernel if square else local
+    return jax.shard_map(body, mesh=mesh, in_specs=in_specs, out_specs=out_specs, check_vma=False)

time: 272 us -> 142 us (0.52)
  Pallas kernels: 0 us -> 138 us
  waiting for transfers between devices: 87.4 us -> 0 us
  matrix products: 56 us -> 0 us
  blocking collectives: 48.4 us -> 0 us
  local copies, waits for them, and re-layouts: 42.6 us -> 2.26 us
  other arithmetic: 19 us -> 0 us
  between operations: 13.2 us -> 0.01 us
  starting transfers between devices: 5.23 us -> 0 us
    pallas_call x0 -> x1, Pallas kernels: none -> 138 us  [one_kernel(): pl.pallas_call(functools.partial(fused, S, H, NS), out_shape=jax.ShapeDty...]
    dot_general x6 -> x0, matrix products: 56 us -> none  [the longest x3 34 us: fold_rows(): return jnp.dot(source, shard_rows, preferred_element_type=jnp.float32)]
    all_gather x5 -> x0, waiting for transfers between devices: 54.2 us -> none  [the longest x1 34.8 us: local(): lax.all_gather(w_value, 'seq', axis=0, tiled=True)]
    all_to_all x1 -> x0, blocking collectives: 48.4 us -> none  [local(): lax.all_to_all(wide_rows, 'head', split_axis=1, concat_axis=0, tiled=True)]
    ppermute x1 -> x0, waiting for transfers between devices: 31.1 us -> none  [passed_along(): return lax.ppermute(block, axis, route)]
    reshape x3 -> x0, local copies, waits for them, and re-layouts: 14.2 us -> none  [the longest x1 6.99 us: local(): key_sum.astype(jnp.bfloat16)]
    gather x1 -> x0, local copies, waits for them, and re-layouts: 13 us -> none  [local(): retrieved = jnp.take(neighbor_bank, slots, axis=0)]
    unnamed x10 -> x1, local copies, waits for them, and re-layouts: 12.1 us -> 2.26 us
  transfers between devices with their start and end apart: 6 -> 0, of which waited for: 5 -> 0; matrix products, arithmetic and copies ran while one was open for 37% -> 0% of each run, Pallas kernels for 0% -> 0%
where the time goes in v1:
time: 142 us; the launch traced here: 140 us
  Pallas kernels  138 us (97%)
  local copies, waits for them, and re-layouts  2.26 us (2%)
    pallas_call x1, Pallas kernels, one_kernel(): pl.pallas_call(functools.partial(fused, S, H, NS), out_shape=jax.ShapeDty...  138 us

profile of v1, /device:TPU:0, one launch (start us, length us, event | category | flops | bytes accessed | tf_op | source)
XLA Modules:
  0.0 139.9 jit_solution(6295576469213973643)
XLA Ops:
  0.0 137.6 %shard_map.73 = bf16[1024,512]{1,0:T(8,128)(2,1)} custom-call(bf16[1024,2048]{1,0:T(8,128)(2,1)} %tokens.1, bf16[16,256,2048]{2,1,0:T(8,128)(2,1)} %bank.1, s32[16]{0:T(128)} %slots.1, bf16[512,512]{1,0:T(8,128)(2,1)} %w_query.1, bf16[512,512]{1,0:T(8,128)(2,1)} %w_key.1, bf16[512,512]{1,0:T(8,128)(2,1)} %w_value.1, bf16[4,128,512]{2,1,0:T(8,128)(2,1)} %bitcast.1), custom_call_target="tpu_custom_call" | custom-call | tf_op jit(solution)/shard_map/pallas_call | solution.py:340
  137.6 2.3 %copy.9 = bf16[1024,512]{1,0:T(8,128)(2,1)} copy(bf16[1024,512]{1,0:T(8,128)(2,1)} %shard_map.73) | data formatting | bytes 2097152

commit v2 on v1

--- a/solution.py
+++ b/solution.py
@@ -16,7 +16,7 @@
 def fused(S, H, NS, tokens, bank, slots, w_query, w_key, w_value, w_out, out,
           G, WO, tok, normed, rows_in, kv, qb, halo_out, halo_in, att_own, att, acc,
           ld_sem, wl_sem, zr, xr, send_r, send_l, send_x, halo_s, halo_r,
-          att_s, att_r, att_l, wo_s, wo_r, wo_xs, wo_xr, wo_l):
+          att_s, att_r, att_l, wo_s, wo_r, wo_l):
     s, h, b = lax.axis_index("seq"), lax.axis_index("head"), lax.axis_index("batch")
     nblk, nrow, D = bank.shape
     T = tokens.shape[0]
@@ -58,6 +58,8 @@
     pl.semaphore_wait(barrier, S * H)
 
     def chunk(t, origin, half):
+        if isinstance(t, int) and t == NS:
+            return wo_part(origin, half)
         return G.at[t, pl.ds(origin * RS + half * RH, RH), :]
 
     def right(t, origin):
@@ -103,13 +105,8 @@
     def wo_part(origin, half):
         return WO.at[:, pl.ds(origin * CW + half * WH, WH), :]
 
-    def wo_send(dest):
-        return rcopy(w_out.at[:, pl.ds(b * WH, WH), :], wo_part(h, b), wo_s.at[dest], wo_r.at[h],
-                     dev(dest, s, b))
-
-    def wo_twin(origin, half):
-        return rcopy(wo_part(origin, half), wo_part(origin, half), wo_xs.at[origin], wo_xr.at[origin],
-                     dev(s, h, 1 - b))
+    def wo_turn(origin, device):
+        return rcopy(w_out.at[:, pl.ds(b * WH, WH), :], wo_part(origin, b), wo_s, wo_r, device)
 
     wo_own = pltpu.make_async_copy(w_out, WO.at[:, pl.ds(h * CW, CW), :], wo_l)
 
@@ -155,7 +152,16 @@
 
     for c in w_loads:
         c.wait()
+    @pl.when(h != s)
+    def _():
+        wo_turn(h, dev(h, s, b)).start()
+
+    @pl.when(h == s)
+    def _():
+        wo_own.start()
+        wo_own.wait()
     send_own(0)
+    send_own(1)
 
     @pl.when(s == 0)
     def _():
@@ -170,41 +176,26 @@
         return 0
     lax.fori_loop(0, nblk, norm, 0)
 
-    @pl.when(h == s)
-    def _():
-        wo_own.start()
     for c in bank_loads:
         c.wait()
 
     group = max(g for g in range(1, 6) if (nblk - 1) % g == 0)
 
     def stage(t, _):
-        @pl.when(t < NS - 1)
-        def _():
-            send_own(t + 1)
-
-        @pl.when(t < S)
-        def _():
-            dest = lax.rem(t * (S - 1), S)
-
-            @pl.when(jnp.logical_or(dest != s, h != s))
-            def _():
-                wo_send(dest).start()
+        @pl.when(t < NS - 2)
+        def _():
+            send_own(t + 2)
 
         @pl.when(t < NS)
         def _():
             relay(t, 1)
 
-        @pl.when(t == NS)
-        def _():
-            for o in range(H):
-                @pl.when(jnp.logical_or(s != h, h != o))
+        @pl.when(t > 0)
+        def _():
+            for o in range(S):
+                @pl.when(s != o)
                 def _():
-                    rcopy(wo_part(o, b), wo_part(o, b), wo_s.at[0], wo_r.at[o], dev(s, h, 1 - b)).wait_recv()
-                    wo_twin(o, b).start()
-
-        @pl.when(t > 0)
-        def _():
+                    twin(t - 1, o, 1 - b).wait_recv()
             project(t - 1, 0, steps // 2)
 
         @pl.when(t < NS)
@@ -226,6 +217,19 @@
         def _():
             for d in range(3, S):
                 relay(t, d)
+
+        @pl.when(t == 0)
+        def _():
+            @pl.when(h != s)
+            def _():
+                wo_turn(s, dev(h, s, b)).wait_recv()
+                twin(NS, s, b).start()
+            send_own(NS)
+
+        for d in range(1, S):
+            @pl.when(t == d)
+            def _():
+                relay(NS, d)
 
         @pl.when(t > 0)
         def _():
@@ -249,24 +253,14 @@
                 att_send(u, k).start()
             att_here(u).start()
 
-        @pl.when(t < NS)
-        def _():
-            for o in range(S):
-                @pl.when(s != o)
-                def _():
-                    twin(t, o, 1 - b).wait_recv()
         return 0
 
     lax.fori_loop(0, NS + 1, stage, 0)
 
-    for o in range(H):
-        @pl.when(jnp.logical_or(s != h, h != o))
-        def _():
-            wo_twin(o, 1 - b).wait_recv()
-
-    @pl.when(h == s)
-    def _():
-        wo_own.wait()
+    for o in range(S):
+        @pl.when(jnp.logical_or(s != o, h != s))
+        def _():
+            twin(NS, o, 1 - b).wait_recv()
 
     tile = T // 4
 
@@ -296,7 +290,7 @@
         return 0
     lax.fori_loop(0, NS, fold, 0)
 
-    def drain(t, _):
+    def drain_weights(t):
         for d in range(S):
             @pl.when(jnp.logical_and(s >= d, s < S - 1))
             def _():
@@ -309,6 +303,9 @@
             @pl.when(s != o)
             def _():
                 twin(t, o, b).wait_send()
+
+    def drain(t, _):
+        drain_weights(t)
 
         @pl.when(s < S - 1)
         def _():
@@ -317,14 +314,12 @@
             att_send(t, k).wait_send()
         return 0
     lax.fori_loop(0, NS, drain, 0)
-    for dest in range(S):
-        @pl.when(jnp.logical_or(dest != s, h != s))
-        def _():
-            wo_send(dest).wait_send()
-    for o in range(H):
-        @pl.when(jnp.logical_or(s != h, h != o))
-        def _():
-            wo_twin(o, b).wait_send()
+    drain_weights(NS)
+
+    @pl.when(h != s)
+    def _():
+        twin(NS, s, b).wait_send()
+        wo_turn(h, dev(h, s, b)).wait_send()
 
 
 def one_kernel(tokens, neighbor_bank, slots, w_query, w_key, w_value, w_out):
@@ -357,10 +352,10 @@
             pltpu.VMEM((T, out_cols), F32),
             dma((nblk + 1,)),
             dma((3 * NS,)),
-            dma((NS, S)), dma((NS, S)), dma((NS, S)), dma((NS, S)), dma((NS, S)),
+            dma((NS + 1, S)), dma((NS + 1, S)), dma((NS + 1, S)), dma((NS + 1, S)), dma((NS + 1, S)),
             dma((NS,)), dma((NS,)),
             dma((NS, 3)), dma((NS, 3)), dma((NS,)),
-            dma((S,)), dma((H,)), dma((H,)), dma((H,)), dma,
+            dma, dma, dma,
         ],
         compiler_params=pltpu.CompilerParams(
             collective_id=0, has_side_effects=True, vmem_limit_bytes=63 * 1024 * 1024),

time: 142 us -> 131 us (0.923)
  Pallas kernels: 138 us -> 127 us
    pallas_call x1, Pallas kernels: 138 us -> 127 us  [one_kernel(): pl.pallas_call(functools.partial(fused, S, H, NS), out_shape=jax.ShapeDty...]
where the time goes in v2:
time: 131 us; the launch traced here: 130 us
  Pallas kernels  127 us (97%)
  local copies, waits for them, and re-layouts  2.26 us (2%)
    pallas_call x1, Pallas kernels, one_kernel(): pl.pallas_call(functools.partial(fused, S, H, NS), out_shape=jax.ShapeDty...  127 us

profile of v2, /device:TPU:0, one launch (start us, length us, event | category | flops | bytes accessed | tf_op | source)
XLA Modules:
  0.0 129.6 jit_solution(10294131557726495689)
XLA Ops:
  0.0 127.4 %shard_map.73 = bf16[1024,512]{1,0:T(8,128)(2,1)} custom-call(bf16[1024,2048]{1,0:T(8,128)(2,1)} %tokens.1, bf16[16,256,2048]{2,1,0:T(8,128)(2,1)} %bank.1, s32[16]{0:T(128)} %slots.1, bf16[512,512]{1,0:T(8,128)(2,1)} %w_query.1, bf16[512,512]{1,0:T(8,128)(2,1)} %w_key.1, bf16[512,512]{1,0:T(8,128)(2,1)} %w_value.1, bf16[4,128,512]{2,1,0:T(8,128)(2,1)} %bitcast.1), custom_call_target="tpu_custom_call" | custom-call | tf_op jit(solution)/shard_map/pallas_call | solution.py:335
  127.4 2.3 %copy.9 = bf16[1024,512]{1,0:T(8,128)(2,1)} copy(bf16[1024,512]{1,0:T(8,128)(2,1)} %shard_map.73) | data formatting | bytes 2097152
